TPU v7x, 128 devices: a whole 4x4x4 slice. The times are simulated.
128 devices in a mesh: seq: 32 (over y, z, core), head: 4 (over x).
Axes of the slice: x: 4, y: 4, z: 4, core: 2. Of those that a mesh axis runs over, the one named last changes fastest.
Arguments:
- queries: bfloat16 [16384, 4096], P('seq', 'head'), may hold values from -5 to 5
- keys: bfloat16 [16384, 1024], P('seq', 'head'), may hold values from -5 to 5
- values: bfloat16 [16384, 1024], P('seq', 'head'), may hold values from -5 to 5
- doc_lengths: int32 [64], replicated, may hold values from 1 to 2048, 16384 in all
- out_weight: bfloat16 [4096, 4096], P('head', 'seq'), may hold values from -0.1875 to 0.1875
Outputs:
- mixed: bfloat16 [16384, 4096], P('seq', 'head')
Inputs may be any that keep to these rules, and one draw needn't show every extreme that they name: `doc_lengths`: the lengths sum to 16384, and one document is exactly 2048 tokens long.
All inputs are finite; a program needn't handle non-finite values.
Results may differ from a plain program's by a relative error of at most 0.012.
Values may be sent and summed in bfloat16 or wider, within the bound.
A program may use at most 128 MiB of HBM per device.

v0:
```python
import math

import jax
import jax.numpy as jnp
from jax import lax
from jax.sharding import PartitionSpec as P

HQ = 32
KV = 8
DH = 128
REACH = 4


def from_behind(block, axis, distance):
    devices = range(lax.axis_size(axis))
    route = [(i - distance, i) for i in devices if i - distance in devices]
    return lax.ppermute(block, axis, route)


def doc_index(positions, starts):
    return jnp.sum((starts[None, :] <= positions[:, None]).astype(jnp.int32), axis=1) - 1


def body(queries, keys, values, doc_lengths, out_weight):
    local_rows = queries.shape[0]
    kv_local = keys.shape[1] // DH
    group_size = HQ // KV
    temper = DH ** (-0.5)
    starts = jnp.cumsum(doc_lengths) - doc_lengths
    q_first = lax.axis_index("seq") * local_rows
    q_pos = q_first + jnp.arange(local_rows, dtype=jnp.int32)
    q_doc = doc_index(q_pos, starts)
    q_heads = queries.reshape(local_rows, kv_local, group_size, DH)

    def attend(carry, piece, piece_start):
        key_piece, value_piece = piece
        key_count = key_piece.shape[0]
        block_len = math.gcd(key_count, 512)
        num_blocks = key_count // block_len
        key_blocks = key_piece.reshape(num_blocks, block_len, kv_local, DH)
        value_blocks = value_piece.reshape(num_blocks, block_len, kv_local, DH)
        block_starts = piece_start + block_len * jnp.arange(num_blocks, dtype=jnp.int32)

        def one_block(state, entry):
            key_block, value_block, block_first = entry
            k_pos = block_first + jnp.arange(block_len, dtype=jnp.int32)
            k_doc = doc_index(k_pos, starts)
            needed = (block_first >= 0) & (block_first <= q_pos[-1]) & (k_doc[-1] >= q_doc[0])

            def update(inner):
                row_max, row_sum, accum = inner
                scores = (
                    jnp.einsum(
                        "qkgd,nkd->kgqn", q_heads, key_block, preferred_element_type=jnp.float32
                    )
                    * temper
                )
                allowed = (k_doc[None, :] == q_doc[:, None]) & (k_pos[None, :] <= q_pos[:, None])
                scores = jnp.where(allowed[None, None], scores, jnp.float32(-1e30))
                new_max = jnp.maximum(row_max, jnp.max(scores, axis=-1))
                probs = jnp.where(
                    allowed[None, None], jnp.exp(scores - new_max[..., None]), jnp.float32(0.0)
                )
                fading = jnp.exp(row_max - new_max)
                row_sum = row_sum * fading + jnp.sum(probs, axis=-1)
                weights = probs.astype(jnp.bfloat16)
                accum = accum * fading[..., None] + jnp.einsum(
                    "kgqn,nkd->kgqd", weights, value_block, preferred_element_type=jnp.float32
                )
                return (new_max, row_sum, accum)

            def unchanged(inner):
                return inner

            return (lax.cond(needed, update, unchanged, state), None)

        carry, _ = lax.scan(one_block, carry, (key_blocks, value_blocks, block_starts))
        return carry

    initial = (
        jnp.full((kv_local, group_size, local_rows), -1e30, jnp.float32),
        jnp.zeros((kv_local, group_size, local_rows), jnp.float32),
        jnp.zeros((kv_local, group_size, local_rows, DH), jnp.float32),
    )
    final = attend(initial, (keys, values), q_first)
    paired = jnp.stack((keys, values))
    for offset in range(REACH):
        paired = from_behind(paired, "seq", 1)
        final = attend(final, (paired[0], paired[1]), q_first - (offset + 1) * local_rows)
    row_max, row_sum, accum = final
    attn = (accum / row_sum[..., None]).astype(jnp.bfloat16)
    attn = jnp.transpose(attn, (2, 0, 1, 3)).reshape(local_rows, kv_local * group_size * DH)
    partial_terms = jnp.dot(
        attn,
        lax.all_gather(out_weight, "seq", axis=1, tiled=True),
        preferred_element_type=jnp.float32,
    )
    return lax.psum_scatter(
        partial_terms.astype(jnp.bfloat16), "head", scatter_dimension=1, tiled=True
    )


def solution(mesh):
    return jax.shard_map(
        body,
        mesh=mesh,
        in_specs=(P("seq", "head"), P("seq", "head"), P("seq", "head"), P(), P("head", "seq")),
        out_specs=P("seq", "head"),
        check_vma=False,
    )
```

profile of v0, /device:TPU:1, one launch (start us, length us, event | category | flops | bytes accessed | tf_op | source)
XLA Modules:
  0.0 184.9 jit_solution(12124513469973427911)
XLA Ops:
  6.5 0.0 all-gather.2.cloned.1.call-start
  6.5 0.7 all-gather.2.cloned.1.call-update
  7.3 0.0 reduce-scatter.2.cloned.1.call-start
  7.3 1.1 copy.53
  8.4 1.1 copy.55
  9.5 0.0 copy-start
  9.5 0.1 pad_maximum_fusion
  9.6 4.9 %collective-permute-start = (bf16[2,512,256]{1,2,0:T(8,128)(2,1)S(1)}, bf16[2,512,256]{1,2,0:T(8,128)(2,1)S(1)}, u32[]{:S(2)}, u32[]{:S(2)}) collective-permute-start(bf16[2,512,256]{1,2,0:T(8,128)(2,1)S(1)} %pad_maximum_fusion), channel_id=1, source_target_pairs={{0,4},{4,8},{8,12},{12,16},{16,20},{20,24},{24,28},{28,32},{32,36}... | collective-permute-start | bytes 1572872 | tf_op jit(solution)/shard_map/ppermute | solution.py:17
  14.5 0.7 copy.52
  15.3 0.1 reduce-window.9
  15.4 0.1 reduce
  15.5 0.7 sub.95
  16.1 4.5 %collective-permute-done = bf16[2,512,256]{1,2,0:T(8,128)(2,1)S(1)} collective-permute-done((bf16[2,512,256]{1,2,0:T(8,128)(2,1)S(1)}, bf16[2,512,256]{1,2,0:T(8,128)(2,1)S(1)}, u32[]{:S(2)}, u32[]{:S(2)}) %collective-permute-start) | collective-permute-done | bytes 524320 | tf_op jit(solution)/shard_map/ppermute | solution.py:17
  20.6 0.0 copy-start.3
  20.6 4.4 %collective-permute-start.1 = (bf16[2,512,256]{1,2,0:T(8,128)(2,1)S(1)}, bf16[2,512,256]{1,2,0:T(8,128)(2,1)S(1)}, u32[]{:S(2)}, u32[]{:S(2)}) collective-permute-start(bf16[2,512,256]{1,2,0:T(8,128)(2,1)S(1)} %collective-permute-done), channel_id=1, source_target_pairs={{0,4},{4,8},{8,12},{12,16},{16,20},{20,24},{24,28},{28,32},{32,36}... | collective-permute-start | bytes 1572872 | tf_op jit(solution)/shard_map/ppermute | solution.py:17
  25.0 0.2 convert_reduce_fusion
  25.2 7.3 %collective-permute-done.1 = bf16[2,512,256]{1,2,0:T(8,128)(2,1)S(1)} collective-permute-done((bf16[2,512,256]{1,2,0:T(8,128)(2,1)S(1)}, bf16[2,512,256]{1,2,0:T(8,128)(2,1)S(1)}, u32[]{:S(2)}, u32[]{:S(2)}) %collective-permute-start.1) | collective-permute-done | bytes 524320 | tf_op jit(solution)/shard_map/ppermute | solution.py:17
  32.5 0.0 copy-start.2
  32.5 4.4 %collective-permute-start.2 = (bf16[2,512,256]{1,2,0:T(8,128)(2,1)S(1)}, bf16[2,512,256]{1,2,0:T(8,128)(2,1)}, u32[]{:S(2)}, u32[]{:S(2)}) collective-permute-start(bf16[2,512,256]{1,2,0:T(8,128)(2,1)S(1)} %collective-permute-done.1), channel_id=1, source_target_pairs={{0,4},{4,8},{8,12},{12,16},{16,20},{20,24},{24,28},{28,32},{32,36}... | collective-permute-start | bytes 1572872 | tf_op jit(solution)/shard_map/ppermute | solution.py:17
  36.9 6.1 %collective-permute-done.2 = bf16[2,512,256]{1,2,0:T(8,128)(2,1)} collective-permute-done((bf16[2,512,256]{1,2,0:T(8,128)(2,1)S(1)}, bf16[2,512,256]{1,2,0:T(8,128)(2,1)}, u32[]{:S(2)}, u32[]{:S(2)}) %collective-permute-start.2) | collective-permute-done | bytes 524320 | tf_op jit(solution)/shard_map/ppermute | solution.py:17
  43.0 4.5 %collective-permute-start.3 = (bf16[2,512,256]{1,2,0:T(8,128)(2,1)}, bf16[2,512,256]{1,2,0:T(8,128)(2,1)}, u32[]{:S(2)}, u32[]{:S(2)}) collective-permute-start(bf16[2,512,256]{1,2,0:T(8,128)(2,1)} %collective-permute-done.2), channel_id=1, source_target_pairs={{0,4},{4,8},{8,12},{12,16},{16,20},{20,24},{24,28},{28,32},{32,36}... | collective-permute-start | bytes 1572872 | tf_op jit(solution)/shard_map/ppermute | solution.py:17
  47.5 0.6 fusion.68
  48.1 0.6 slice.72
  51.8 0.6 slice.73
  53.6 0.6 slice.75
  55.4 0.7 slice.76
  57.3 0.6 slice.77
  60.2 1.5 copy.54
  61.7 0.0 copy-done
  61.7 0.0 copy-done.3
  61.7 0.0 copy-done.2
  61.7 0.1 broadcast_in_dim.152
  61.9 7.7 %conditional.5 = ((f32[2,4,512]{2,1,0:T(4,128)S(1)}, f32[2,4,512]{2,1,0:T(4,128)S(1)}, f32[2,4,512,128]{3,2,1,0:T(8,128)S(1)})) conditional(s32[]{:T(128)} %convert_element_type.72, (f32[2,4,512]{2,1,0:T(4,128)S(1)}, f32[2,4,512]{2,1,0:T(4,128)S(1)}, f32[2,4,512,128]{3,2,1,0:T(8,128)S(1)}) %tuple.52, (s32[512]{0:T(512)S(1)}, s32[512]{0:T(512)S(1)}, ...), branch_computations={%region_6.7_spmd, %region_7.10_spmd} | conditional | flops 1102848000 | bytes 33296444 | solution.py:75
  61.9 0.3 compare_and_fusion
  62.2 0.0 copy-start.1
  62.2 1.6 fusion
  63.8 2.0 %fusion.2 = f32[2,4,512]{2,1,0:T(4,128)S(1)} fusion(f32[2,512,512,4]{2,1,3,0:T(8,128)S(1)} %get-tuple-element.540, f32[2,4,512]{2,1,0:T(4,128)S(1)} %max.11, pred[512,512]{0,1:T(8,128)(4,1)S(1)} %compare_and_fusion), kind=kLoop, calls=%fused_computation.4 | loop fusion | flops 10481664 | bytes 8683520 | tf_op jit(solution)/shard_map/while/body/eval_jaxpr/cond/branch_1_fun/reduce_sum | solution.py:65
  65.9 0.0 copy-done.1
  65.9 3.6 %multiply_add_fusion = f32[2,4,512,128]{3,2,1,0:T(8,128)S(1)} fusion(f32[2,4,512,128]{3,2,1,0:T(8,128)S(1)} %get-tuple-element.301, f32[2,512,512,4]{2,1,3,0:T(8,128)S(1)} %get-tuple-element.540, f32[2,4,512]{2,1,0:T(4,128)S(1)} %max.11, pred[512,512]{0,1:T(8,128)(4,1)S(1)} %compare_and_fusion, f32[2,4,512]{2,1,0:T(4,128)S(1)} %bitcast.225, ...), kind=kOutput, calls=%fused_computation.7 | convolution fusion | flops 548405248 | bytes 13139968 | tf_op jit(solution)/shard_map/while/body/eval_jaxpr/cond/branch_1_fun/kgqn,nkd->kgqd/dot_general | solution.py:67
  69.6 1.1 fusion.67
  70.7 8.0 %conditional.6 = ((f32[2,4,512]{2,1,0:T(4,128)S(1)}, f32[2,4,512]{2,1,0:T(4,128)S(1)}, f32[2,4,512,128]{3,2,1,0:T(8,128)S(1)})) conditional(s32[]{:T(128)} %convert_element_type.71, (f32[2,4,512]{2,1,0:T(4,128)S(1)}, f32[2,4,512]{2,1,0:T(4,128)S(1)}, f32[2,4,512,128]{3,2,1,0:T(8,128)S(1)}) %get-tuple-element.599, (s32[512]{0:T(512)S(1)}, ...), branch_computations={%region_10.11_spmd, %region_11.14_spmd} | conditional | flops 1102848000 | bytes 32251936 | solution.py:75
  71.1 0.3 compare_and_fusion.1
  71.3 1.6 fusion.14
  73.0 2.0 %fusion.16 = f32[2,4,512]{2,1,0:T(4,128)S(1)} fusion(f32[2,512,512,4]{2,1,3,0:T(8,128)S(1)} %get-tuple-element.542, f32[2,4,512]{2,1,0:T(4,128)S(1)} %max.12, pred[512,512]{0,1:T(8,128)(4,1)S(1)} %compare_and_fusion.1), kind=kLoop, calls=%fused_computation.21 | loop fusion | flops 10481664 | bytes 8683520 | tf_op jit(solution)/shard_map/while/body/eval_jaxpr/cond/branch_1_fun/reduce_sum | solution.py:65
  75.0 3.7 %multiply_add_fusion.2 = f32[2,4,512,128]{3,2,1,0:T(8,128)S(1)} fusion(f32[2,4,512,128]{3,2,1,0:T(8,128)S(1)} %get-tuple-element.332, f32[2,512,512,4]{2,1,3,0:T(8,128)S(1)} %get-tuple-element.542, f32[2,4,512]{2,1,0:T(4,128)S(1)} %max.12, pred[512,512]{0,1:T(8,128)(4,1)S(1)} %compare_and_fusion.1, f32[2,4,512]{2,1,0:T(4,128)S(1)} %bitcast.226, ...), kind=kOutput, calls=%fused_computation.24 | convolution fusion | flops 548405248 | bytes 13139968 | tf_op jit(solution)/shard_map/while/body/eval_jaxpr/cond/branch_1_fun/kgqn,nkd->kgqd/dot_general | solution.py:67
  78.7 1.2 fusion.66
  79.9 8.6 %conditional.8 = ((f32[2,4,512]{2,1,0:T(4,128)S(1)}, f32[2,4,512]{2,1,0:T(4,128)S(1)}, f32[2,4,512,128]{3,2,1,0:T(8,128)S(1)})) conditional(s32[]{:T(128)} %convert_element_type.67, (f32[2,4,512]{2,1,0:T(4,128)S(1)}, f32[2,4,512]{2,1,0:T(4,128)S(1)}, f32[2,4,512,128]{3,2,1,0:T(8,128)S(1)}) %get-tuple-element.601, (s32[512]{0:T(512)S(1)}, ...), branch_computations={%region_18.19_spmd, %region_19.22_spmd} | conditional | flops 1102848512 | bytes 33304612 | solution.py:75
  88.5 0.0 collective-permute-done.3
  88.5 1.8 conditional.9
  88.5 1.8 copy.110
  90.4 1.9 %divide_convert_fusion = bf16[2,4,512,128]{2,3,1,0:T(8,128)(2,1)S(1)} fusion(f32[2,4,512,128]{2,3,1,0:T(8,128)} %get-tuple-element.523, f32[2,4,512]{2,1,0:T(4,128)S(1)} %get-tuple-element.404), kind=kLoop, calls=%fused_computation.82 | loop fusion | flops 1048576 | bytes 3162112 | tf_op jit(solution)/shard_map/convert_element_type | solution.py:91
  92.2 0.0 all-gather.2.cloned.1.call-done
  92.3 9.5 %convolution_convert_fusion = bf16[512,4096]{1,0:T(8,128)(2,1)} fusion(bf16[512,1024]{0,1:T(8,128)(2,1)S(1)} %bitcast.193, bf16[1024,4096]{1,0:T(8,128)(2,1)} %all-gather.2.cloned.1.call-done), kind=kOutput, calls=%fused_computation.81 | convolution fusion | flops 4297064448 | bytes 13631488 | tf_op jit(solution)/shard_map/dot_general | solution.py:93
  101.7 0.0 reduce-scatter.2.cloned.1.call-update
  101.8 76.1 %reduce-scatter.2.cloned.1.call-done = bf16[512,1024]{1,0:T(8,128)(2,1)} async-done(((bf16[512,4096]{1,0:T(8,128)(2,1)}), bf16[512,1024]{1,0:T(8,128)(2,1)}) %reduce-scatter.2.cloned.1.call-update) | async-done | bytes 1048592 | tf_op jit(solution)/shard_map/reduce_scatter | solution.py:98
  (20 shorter events, 0.1 us)
Async XLA Ops:
  6.5 85.7 %all-gather.2.cloned.1.call-start = ((), (), s32[]{:S(2)}) async-start(), calls=%async_computation.1 | async-start | bytes 8650752 | tf_op jit(solution)/shard_map/all_gather | solution.py:95
  7.3 170.6 %reduce-scatter.2.cloned.1.call-start = ((), (), s32[]{:S(2)}) async-start(), calls=%async_computation.2 | async-start | bytes 5242880 | tf_op jit(solution)/shard_map/reduce_scatter | solution.py:98
  9.5 52.2 %copy-start = (bf16[512,256]{0,1:T(8,128)(2,1)}, bf16[512,256]{0,1:T(8,128)(2,1)S(1)}, u32[]{:S(2)}) copy-start(bf16[512,256]{0,1:T(8,128)(2,1)S(1)} %copy.55) | copy-start | bytes 786436
  9.6 11.0 %collective-permute-start = (bf16[2,512,256]{1,2,0:T(8,128)(2,1)S(1)}, bf16[2,512,256]{1,2,0:T(8,128)(2,1)S(1)}, u32[]{:S(2)}, u32[]{:S(2)}) collective-permute-start(bf16[2,512,256]{1,2,0:T(8,128)(2,1)S(1)} %pad_maximum_fusion), channel_id=1, source_target_pairs={{0,4},{4,8},{8,12},{12,16},{16,20},{20,24},{24,28},{28,32},{32,36}... | collective-permute-start | bytes 1572872 | tf_op jit(solution)/shard_map/ppermute | solution.py:17
  20.6 41.1 %copy-start.3 = (bf16[2,512,256]{1,2,0:T(8,128)(2,1)}, bf16[2,512,256]{1,2,0:T(8,128)(2,1)S(1)}, u32[]{:S(2)}) copy-start(bf16[2,512,256]{1,2,0:T(8,128)(2,1)S(1)} %collective-permute-done) | copy-start | bytes 1572868
  20.6 11.9 %collective-permute-start.1 = (bf16[2,512,256]{1,2,0:T(8,128)(2,1)S(1)}, bf16[2,512,256]{1,2,0:T(8,128)(2,1)S(1)}, u32[]{:S(2)}, u32[]{:S(2)}) collective-permute-start(bf16[2,512,256]{1,2,0:T(8,128)(2,1)S(1)} %collective-permute-done), channel_id=1, source_target_pairs={{0,4},{4,8},{8,12},{12,16},{16,20},{20,24},{24,28},{28,32},{32,36}... | collective-permute-start | bytes 1572872 | tf_op jit(solution)/shard_map/ppermute | solution.py:17
  32.5 29.2 %copy-start.2 = (bf16[2,512,256]{1,2,0:T(8,128)(2,1)}, bf16[2,512,256]{1,2,0:T(8,128)(2,1)S(1)}, u32[]{:S(2)}) copy-start(bf16[2,512,256]{1,2,0:T(8,128)(2,1)S(1)} %collective-permute-done.1) | copy-start | bytes 1572868
  32.5 10.5 %collective-permute-start.2 = (bf16[2,512,256]{1,2,0:T(8,128)(2,1)S(1)}, bf16[2,512,256]{1,2,0:T(8,128)(2,1)}, u32[]{:S(2)}, u32[]{:S(2)}) collective-permute-start(bf16[2,512,256]{1,2,0:T(8,128)(2,1)S(1)} %collective-permute-done.1), channel_id=1, source_target_pairs={{0,4},{4,8},{8,12},{12,16},{16,20},{20,24},{24,28},{28,32},{32,36}... | collective-permute-start | bytes 1572872 | tf_op jit(solution)/shard_map/ppermute | solution.py:17
  43.0 45.5 %collective-permute-start.3 = (bf16[2,512,256]{1,2,0:T(8,128)(2,1)}, bf16[2,512,256]{1,2,0:T(8,128)(2,1)}, u32[]{:S(2)}, u32[]{:S(2)}) collective-permute-start(bf16[2,512,256]{1,2,0:T(8,128)(2,1)} %collective-permute-done.2), channel_id=1, source_target_pairs={{0,4},{4,8},{8,12},{12,16},{16,20},{20,24},{24,28},{28,32},{32,36}... | collective-permute-start | bytes 1572872 | tf_op jit(solution)/shard_map/ppermute | solution.py:17
  62.2 3.7 %copy-start.1 = (bf16[512,2,128]{0,2,1:T(8,128)(2,1)S(1)}, bf16[512,2,128]{0,2,1:T(8,128)(2,1)}, u32[]{:S(2)}) copy-start(bf16[512,2,128]{0,2,1:T(8,128)(2,1)} %get-tuple-element.480) | copy-start | bytes 786436 | tf_op jit(solution)/shard_map/while/body/eval_jaxpr/cond
Sparse Core Ops, SparseCore 0:
  9.5 72.2 all-gather.1
  101.9 75.8 reduce-scatter.1
where the time goes:
time: 183 us; the launch traced here: 185 us
  waiting for transfers between devices  94.7 us (52%)
  between operations  22.9 us (13%)
  matrix products  20 us (11%)
  starting transfers between devices  18.2 us (10%)
  local copies, waits for them, and re-layouts  12.4 us (7%)
  loops' own time  9.1 us (5%)
  other arithmetic  7.67 us (4%)
    reduce_scatter x1, waiting for transfers between devices, body(): lax.psum_scatter(partial_terms.astype(jnp.bfloat16), 'head', scatter_dime...  76.1 us
    ppermute x4, starting transfers between devices, from_behind(): return lax.ppermute(block, axis, route)  18.2 us
    ppermute x4, waiting for transfers between devices, from_behind(): return lax.ppermute(block, axis, route)  17.8 us
    dot_general x1, matrix products, body(): jnp.dot(attn, lax.all_gather(out_weight, 'seq', axis=1, tiled=True), pref...  9.48 us
    another operation x5, loops' own time, one_block(): return (lax.cond(needed, update, unchanged, state), None)  9.1 us
    dot_general x2, matrix products, update(): jnp.einsum('kgqn,nkd->kgqd', weights, value_block, preferred_element_type...  7.3 us
    reduce_sum x2, other arithmetic, update(): row_sum = row_sum * fading + jnp.sum(probs, axis=-1)  4.09 us
    unnamed x9, local copies, waits for them, and re-layouts  3.71 us
  transfers between devices with their start and end apart: 6, of which 4 were waited for; matrix products, arithmetic and copies ran while one was open for 17% of the time, Pallas kernels for 0%

commit v1 on v0

v1 whole, which is shorter than its diff:
```python
import jax
import jax.numpy as jnp
from jax import lax
from jax.experimental import pallas as pl
from jax.experimental.pallas import tpu as pltpu
from jax.sharding import PartitionSpec as P

DH = 128
TOK = 512
ROWS = 2560
FAR = 16384.0
LOG2E = 1.4426950408889634
C2 = LOG2E * DH ** -0.5
F32 = jnp.float32
BF16 = jnp.bfloat16
MESH = pl.DeviceIdType.MESH


class Sems:
    def __init__(self, send, recv):
        self.send, self.recv, self.names, self.pending = send, recv, {}, []

    def index(self, name):
        return self.names.setdefault(name, len(self.names))

    def remote(self, name, src, dst, dev):
        i = self.index(name)
        return pltpu.make_async_remote_copy(
            src_ref=src, dst_ref=dst, send_sem=self.send.at[i], recv_sem=self.recv.at[i],
            device_id=dev, device_id_type=MESH)

    def go(self, name, src, dst, dev):
        d = self.remote(name, src, dst, dev)
        d.start()
        self.pending.append(d)
        return d


def kernel(q_ref, k_ref, v_ref, w_ref, len_ref, out_ref,
           qd, qcode, kd, kcode, vd, vrelay, wbuf, abuf, mbuf, acc, oacc, lens,
           loc_sem, send_sem, recv_sem, xs_sem, xr_sem):
    mx = lax.axis_index("head")
    s = lax.axis_index("seq")
    y = s // 8
    z = (s // 2) % 4
    c = s % 2
    sm = Sems(send_sem, recv_sem)

    def dev(seq, head=None):
        return {"seq": seq, "head": mx if head is None else head}

    def at(yy, zz, cc):
        return yy * 8 + zz * 2 + cc

    sib = dev(s + 1 - 2 * c)
    nxt = dev((s + 2) % 32)
    prv = dev((s + 30) % 32)
    zp, zm = dev(at(y, (z + 1) % 4, c)), dev(at(y, (z + 3) % 4, c))
    yp, ym = dev(at((y + 1) % 4, z, c)), dev(at((y + 3) % 4, z, c))
    xp, xm = dev(s, (mx + 1) % 4), dev(s, (mx + 3) % 4)
    p = y * 4 + z
    fwd = dev(((y * 4 + (z + 1) % 4 + 2) % 16) * 2 + c)
    po = (p + 14) % 16
    bwd = dev(at(po // 4, (po + 3) % 4, c))
    swap = {"seq": at(mx, z, c), "head": y}
    off = mx != y
    f1, f2 = z + c * (y - z), y + c * (z - y)

    def along(first, step):
        d1, d2 = (step, 0) if first else (0, step)
        i1, i2 = (f1 + d1) % 4, (f2 + d2) % 4
        yy, zz = i2 + c * (i1 - i2), i1 + c * (i2 - i1)
        return dev(at(yy, zz, c))

    def wblock(d1, d2):
        i1, i2 = (f1 + d1) % 4, (f2 + d2) % 4
        yy, zz = i2 + c * (i1 - i2), i1 + c * (i2 - i1)
        return wbuf.at[c, yy, zz]

    loc = []

    def local(src, dst):
        d = pltpu.make_async_copy(src, dst, loc_sem.at[len(loc)])
        d.start()
        loc.append(d)
        return d

    own = pl.ds(2048, TOK)
    lk = [local(k_ref.at[:, pl.ds(j * DH, DH)], kd.at[j, own]) for j in range(2)]
    lv = [local(v_ref.at[:, pl.ds(j * DH, DH)], vd.at[j, own]) for j in range(2)]
    lq = [local(q_ref.at[:, pl.ds(h * DH, DH)], qd.at[h]) for h in range(8)]

    barrier = pltpu.get_barrier_semaphore()
    for peer in (sib, nxt, prv, zp, zm, yp, ym, xp, xm, fwd, bwd):
        pl.semaphore_signal(barrier, inc=1, device_id=peer, device_id_type=MESH)

    @pl.when(off)
    def _():
        pl.semaphore_signal(barrier, inc=1, device_id=swap, device_id_type=MESH)

    lens[...] = jnp.zeros_like(lens)
    lens[0:1, 0:64] = len_ref[...]
    row = lens[0:1, :].astype(F32)
    i0 = lax.broadcasted_iota(jnp.int32, (DH, DH), 0)
    i1 = lax.broadcasted_iota(jnp.int32, (DH, DH), 1)
    col = jnp.sum(jnp.where(i1 < i0, jnp.broadcast_to(row, (DH, DH)), 0.0), axis=1, keepdims=True)
    start = jnp.sum(jnp.where(i0 == i1, jnp.broadcast_to(col, (DH, DH)), 0.0), axis=0, keepdims=True)
    end = start + row
    first = s * TOK

    @pl.loop(0, ROWS // 256)
    def _(b):
        pos = (first - 2048 + b * 256 + lax.broadcasted_iota(jnp.int32, (256, DH), 0)).astype(F32)
        inside = (pos >= start) & (pos < end)
        kcode[pl.ds(pl.multiple_of(b * 256, 256), 256), :] = jnp.where(inside, 0.0, -FAR).astype(BF16)

    for b in range(2):
        pos = (first + b * 256 + lax.broadcasted_iota(jnp.int32, (256, DH), 0)).astype(F32)
        inside = (pos >= start) & (pos < end)
        qcode[pl.ds(b * 256, 256), :] = jnp.where(inside, 1.0, 0.0).astype(BF16)

    for d in lk + lv:
        d.wait()
    pl.semaphore_wait(barrier, 11 + off.astype(jnp.int32))

    def slot(buf, j, i):
        start_row = (4 - i) * TOK
        if not isinstance(i, int):
            start_row = pl.multiple_of(start_row, TOK)
        return buf.at[j, pl.ds(start_row, TOK)]

    def both(name, j, src, dst, to):
        sm.go(f"{name}k{j}", slot(kd, j, src), slot(kd, j, dst), to)
        sm.go(f"{name}v{j}", slot(vd, j, src), slot(vd, j, dst), to)

    def both_recv(name, j, dst):
        sm.remote(f"{name}k{j}", slot(kd, j, dst), slot(kd, j, dst), sib).wait_recv()
        sm.remote(f"{name}v{j}", slot(vd, j, dst), slot(vd, j, dst), sib).wait_recv()

    def side(name, j, src, dst, when):
        ds = [sm.remote(f"{name}k{j}", slot(kd, j, src), slot(kd, j, dst), sib),
              sm.remote(f"{name}v{j}", slot(vd, j, src), slot(vd, j, dst), sib)]

        @pl.when(when)
        def _():
            for d in ds:
                d.start()
        return ds

    def kv_near(j):
        sm.go(f"relay{j}", slot(vd, j, 0), vrelay.at[j], zm)
        both("near", j, 0, 2, nxt)
        side("d1", j, 0, 1, c == 0)

    def kv_mid(j):
        both_recv("near", j, 2)
        sm.go(f"fark{j}", slot(kd, j, 2), slot(kd, j, 4), nxt)
        sm.remote(f"relay{j}", vrelay.at[j], vrelay.at[j], sib).wait_recv()
        sm.go(f"farv{j}", vrelay.at[j], slot(vd, j, 4), fwd)
        side("d1", j, 2, 1, c == 1)
        side("d2", j, 2, 3, c == 0)

    def kv_last(j):
        sm.remote(f"fark{j}", slot(kd, j, 4), slot(kd, j, 4), sib).wait_recv()
        sm.remote(f"farv{j}", slot(vd, j, 4), slot(vd, j, 4), sib).wait_recv()
        side("d2", j, 4, 3, c == 1)

    ones = jnp.ones((256, DH), BF16)

    def tile(h, j, qc, lo, n, init, diag, last):
        rows = pl.ds(qc * 256, 256)
        qa = jnp.concatenate([qd[h, rows, :], qcode[rows, :]], axis=1)
        ka = jnp.concatenate([kd[j, pl.ds(lo, n), :], kcode[pl.ds(lo, n), :]], axis=1)
        sc = lax.dot_general(qa, ka, (((1,), (1,)), ((), ())), preferred_element_type=F32)
        if diag:
            r = lax.broadcasted_iota(jnp.int32, (256, n), 0)
            u = lax.broadcasted_iota(jnp.int32, (256, n), 1)
            sc = jnp.where(u <= r + qc * 256, sc, -FAR)
        top = jnp.max(sc, axis=1, keepdims=True)
        if init:
            new = jnp.broadcast_to(top, (256, DH))
        else:
            old = mbuf[h, rows, :]
            new = jnp.maximum(old, top)
        pr = jnp.exp2((sc - jnp.concatenate([new] * (n // DH), axis=1)) * C2).astype(BF16)
        va = jnp.concatenate(
            [vd[j, pl.ds(lo, n), :], jnp.concatenate([ones] * (n // 256), axis=0)], axis=1)
        o = jnp.dot(pr, va, preferred_element_type=F32)
        if not init:
            fade = jnp.exp2((old - new) * C2)
            o = o + acc[h, rows, :] * jnp.concatenate([fade, fade], axis=1)
        if last:
            abuf[mx, h, rows, :] = (o[:, :DH] / o[:, DH:]).astype(BF16)
        else:
            mbuf[h, rows, :] = new
            acc[h, rows, :] = o

    def sweep(j, step, after=None):
        @pl.loop(0, 4)
        def _(g):
            h = j * 4 + g
            for qc in range(2):
                if step == 0:
                    tile(h, j, qc, 2048, 256 + 256 * qc, True, True, False)
                elif step == 1:
                    tile(h, j, qc, 1024, 1024, False, False, False)
                else:
                    tile(h, j, qc, 256 * qc, 1024 - 256 * qc, False, False, True)
            if after is not None:
                after(h)

    def xcopy(kind, h, block, lo, n, to):
        ref = abuf.at[block, h, pl.ds(lo, n)]
        return pltpu.make_async_remote_copy(
            src_ref=ref, dst_ref=ref, send_sem=xs_sem.at[kind, h], recv_sem=xr_sem.at[kind, h],
            device_id=to, device_id_type=MESH)

    xl, xr, xo = (mx + 3) % 4, (mx + 1) % 4, (mx + 2) % 4

    def xsend(h):
        xcopy(0, h, mx, 0, TOK, xp).start()
        xcopy(1, h, mx, 0, TOK, xm).start()

    def xrelay(h):
        xcopy(0, h, xl, 0, TOK, xp).wait_recv()
        xcopy(2, h, xl, 0, 256, xp).start()
        xcopy(1, h, xr, 0, TOK, xm).wait_recv()
        xcopy(3, h, xr, 256, 256, xm).start()

    def xdone(h):
        xcopy(2, h, xo, 0, 256, xp).wait_recv()
        xcopy(3, h, xo, 256, 256, xm).wait_recv()

    wt = sm.remote("wt", w_ref, wbuf.at[c, y, z], swap)
    wt_dst = sm.remote("wt", wbuf.at[c, y, z], wbuf.at[c, y, z], swap)
    wl = pltpu.make_async_copy(w_ref, wbuf.at[c, y, z], loc_sem.at[12])

    def w_swap():
        @pl.when(off)
        def _():
            pltpu.make_async_remote_copy(
                src_ref=w_ref, dst_ref=wbuf.at[c, mx, z], send_sem=send_sem.at[sm.index("wt")],
                recv_sem=recv_sem.at[sm.index("wt")], device_id=swap, device_id_type=MESH).start()

        @pl.when(jnp.logical_not(off))
        def _():
            wl.start()

    def w_swapped():
        @pl.when(off)
        def _():
            wt_dst.wait_recv()

        @pl.when(jnp.logical_not(off))
        def _():
            wl.wait()

    def w_side(d1, d2):
        b = wblock(d1, d2)
        sm.go(f"ws{d1}{d2}", b, b, sib)

    def w_send(d1, d2, second):
        b = wblock(d1, d2)
        sm.go(f"w{second}+{d1}", b, b, along(not second, 1))
        sm.go(f"w{second}-{d1}", b, b, along(not second, -1))

    def w_relay(d1, second):
        a, b = ((d1, -1), (d1, 1)) if second else ((-1, 0), (1, 0))
        ra, rb = wblock(*a), wblock(*b)
        sm.remote(f"w{second}+{d1}", ra, ra, sib).wait_recv()
        h = ra.at[pl.ds(0, 512)]
        sm.go(f"wr{second}+{d1}", h, h, along(not second, 1))
        w_side(*a)
        sm.remote(f"w{second}-{d1}", rb, rb, sib).wait_recv()
        h = rb.at[pl.ds(512, 512)]
        sm.go(f"wr{second}-{d1}", h, h, along(not second, -1))
        w_side(*b)

    def w_far(d1, second):
        o = (d1, 2) if second else (2, 0)
        b = wblock(*o)
        sm.remote(f"wr{second}+{d1}", b.at[pl.ds(0, 512)], b.at[pl.ds(0, 512)], sib).wait_recv()
        sm.remote(f"wr{second}-{d1}", b.at[pl.ds(512, 512)], b.at[pl.ds(512, 512)], sib).wait_recv()
        w_side(*o)

    kv_near(0)
    w_swap()
    for d in lq:
        d.wait()
    sweep(0, 0)
    sweep(1, 0)
    kv_mid(0)
    kv_near(1)
    w_swapped()
    w_side(0, 0)
    w_send(0, 0, 0)
    w_send(0, 0, 1)
    both_recv("d1", 0, 1)
    sweep(0, 1)
    kv_last(0)
    both_recv("d2", 0, 3)
    sweep(0, 2, xsend)
    kv_mid(1)
    w_relay(0, 0)
    w_send(-1, 0, 1)
    w_send(1, 0, 1)
    both_recv("d1", 1, 1)
    sweep(1, 1)
    w_far(0, 0)
    w_send(2, 0, 1)
    w_relay(0, 1)
    xrelay(0)
    xrelay(1)
    kv_last(1)
    both_recv("d2", 1, 3)
    sweep(1, 2, xsend)

    xrelay(2)
    xrelay(3)
    w_far(0, 1)
    w_relay(-1, 1)
    w_relay(1, 1)
    xrelay(4)
    xrelay(5)
    w_far(-1, 1)
    w_far(1, 1)
    w_relay(2, 1)
    xrelay(6)
    xrelay(7)
    w_far(2, 1)
    ws_dst = [(d1, d2) for d1 in (0, -1, 1, 2) for d2 in (0, -1, 1, 2)]
    other = 1 - c
    for d1, d2 in ws_dst:
        sm.remote(f"ws{d1}{d2}", wbuf.at[other, 0, 0], wbuf.at[other, 0, 0], sib).wait_recv()

    def project(block, j, init, last=False):
        @pl.loop(0, 8)
        def _(t):
            cc, r = t // 4, pl.ds(pl.multiple_of((t % 4) * 128, 128), 128)
            a = jnp.concatenate([abuf[block, j * 4 + g, r, :] for g in range(4)], axis=1)
            w = jnp.concatenate([wbuf[cc, block, b, pl.ds(j * 512, 512), :] for b in range(4)], axis=1)
            o = jnp.dot(a, w, preferred_element_type=F32)
            if not init:
                o = o + oacc[cc, r, :]
            oacc[cc, r, :] = o

    project(mx, 0, True)
    project(mx, 1, False)
    for j in range(2):
        project(xl, j, False)
        project(xr, j, False)
    for h in range(8):
        xdone(h)
    for j in range(2):
        project(xo, j, False)
    for cc in range(2):
        for b in range(4):
            out_ref[:, (2 * b + cc) * 128:(2 * b + cc + 1) * 128] = oacc[cc, :, b * 128:(b + 1) * 128].astype(BF16)

    for d in sm.pending:
        d.wait_send()
    for j in range(2):
        for kv in "kv":
            buf = kd if kv == "k" else vd
            r = slot(buf, j, 0)
            sm.remote(f"d1{kv}{j}", r, r, sib).wait_send()
            sm.remote(f"d2{kv}{j}", r, r, sib).wait_send()

    @pl.when(off)
    def _():
        wt.wait_send()
    for h in range(8):
        xcopy(0, h, mx, 0, TOK, xp).wait_send()
        xcopy(1, h, mx, 0, TOK, xm).wait_send()
        xcopy(2, h, xl, 0, 256, xp).wait_send()
        xcopy(3, h, xr, 256, 256, xm).wait_send()


def body(queries, keys, values, doc_lengths, out_weight):
    hbm = pl.BlockSpec(memory_space=pl.ANY)
    vmem = pl.BlockSpec(memory_space=pltpu.VMEM)
    return pl.pallas_call(
        kernel,
        out_shape=jax.ShapeDtypeStruct((TOK, 1024), BF16),
        in_specs=[hbm, hbm, hbm, hbm, vmem],
        out_specs=vmem,
        scratch_shapes=[
            pltpu.VMEM((8, TOK, DH), BF16),
            pltpu.VMEM((TOK, DH), BF16),
            pltpu.VMEM((2, ROWS, DH), BF16),
            pltpu.VMEM((ROWS, DH), BF16),
            pltpu.VMEM((2, ROWS, DH), BF16),
            pltpu.VMEM((2, TOK, DH), BF16),
            pltpu.VMEM((2, 4, 4, 1024, DH), BF16),
            pltpu.VMEM((4, 8, TOK, DH), BF16),
            pltpu.VMEM((8, TOK, DH), F32),
            pltpu.VMEM((8, TOK, 2 * DH), F32),
            pltpu.VMEM((2, TOK, 512), F32),
            pltpu.VMEM((8, DH), jnp.int32),
            pltpu.SemaphoreType.DMA((13,)),
            pltpu.SemaphoreType.DMA((64,)),
            pltpu.SemaphoreType.DMA((64,)),
            pltpu.SemaphoreType.DMA((4, 8)),
            pltpu.SemaphoreType.DMA((4, 8)),
        ],
        compiler_params=pltpu.CompilerParams(
            collective_id=0, has_side_effects=True, vmem_limit_bytes=60 * 1024 * 1024),
        name="attention_block",
    )(queries, keys, values, out_weight, doc_lengths.reshape(1, 64))


def solution(mesh):
    return jax.shard_map(
        body,
        mesh=mesh,
        in_specs=(P("seq", "head"), P("seq", "head"), P("seq", "head"), P(), P("head", "seq")),
        out_specs=P("seq", "head"),
        check_vma=False,
    )
```

time: 183 us -> 88 us (0.48); the launches traced: 185 us -> 87.8 us
  waiting for transfers between devices: 94.7 us -> 0 us
  Pallas kernels: 0 us -> 85.5 us
  between operations: 22.9 us -> 0.01 us
  matrix products: 20 us -> 0 us
  starting transfers between devices: 18.2 us -> 0 us
  local copies, waits for them, and re-layouts: 12.4 us -> 2.26 us
  loops' own time: 9.1 us -> 0 us
  other arithmetic: 7.67 us -> 0 us
    pallas_call x0 -> x1, Pallas kernels: none -> 85.5 us  [body(): pl.pallas_call(kernel, out_shape=jax.ShapeDtypeStruct((TOK, 1024), BF16),...]
    reduce_scatter x1 -> x0, waiting for transfers between devices: 76.1 us -> none  [body(): lax.psum_scatter(partial_terms.astype(jnp.bfloat16), 'head', scatter_dime...]
    dot_general x5 -> x0, matrix products: 20 us -> none  [the longest x1 9.48 us: body(): jnp.dot(attn, lax.all_gather(out_weight, 'seq', axis=1, tiled=True), pref...]
    ppermute x4 -> x0, starting transfers between devices: 18.2 us -> none  [from_behind(): return lax.ppermute(block, axis, route)]
    ppermute x4 -> x0, waiting for transfers between devices: 17.8 us -> none  [from_behind(): return lax.ppermute(block, axis, route)]
    another operation x5 -> x0, loops' own time: 9.1 us -> none  [one_block(): return (lax.cond(needed, update, unchanged, state), None)]
    slice x8 -> x0, local copies, waits for them, and re-layouts: 5.94 us -> none  [the longest x5 3.07 us: one_block(): k_doc[-1] >= q_doc[0]]
    reduce_sum x3 -> x0, other arithmetic: 4.26 us -> none  [the longest x2 4.09 us: update(): row_sum = row_sum * fading + jnp.sum(probs, axis=-1)]
  transfers between devices with their start and end apart: 6 -> 0, of which waited for: 4 -> 0; matrix products, arithmetic and copies ran while one was open for 17% -> 0% of each run, Pallas kernels for 0% -> 0%
where the time goes in v1:
time: 88 us; the launch traced here: 87.8 us
  Pallas kernels  85.5 us (97%)
  local copies, waits for them, and re-layouts  2.26 us (3%)
    pallas_call x1, Pallas kernels, body(): pl.pallas_call(kernel, out_shape=jax.ShapeDtypeStruct((TOK, 1024), BF16),...  85.5 us
    unnamed x1, local copies, waits for them, and re-layouts  2.26 us

profile of v1, /device:TPU:1, one launch (start us, length us, event | category | flops | bytes accessed | tf_op | source)
XLA Modules:
  0.0 87.8 jit_solution(16538092989513803453)
XLA Ops:
  0.0 85.5 %attention_block.1 = bf16[512,1024]{1,0:T(8,128)(2,1)} custom-call(bf16[512,1024]{1,0:T(8,128)(2,1)} %q_ref.1, bf16[512,256]{1,0:T(8,128)(2,1)} %k_ref.1, bf16[512,256]{1,0:T(8,128)(2,1)} %v_ref.1, bf16[1024,128]{1,0:T(8,128)(2,1)} %w_ref.1, s32[1,64]{1,0:T(1,128)} %bitcast.1), custom_call_target="tpu_custom_call" | custom-call | tf_op jit(solution)/shard_map/attention_block/pallas_call | solution.py:382
  85.5 2.3 %copy.7 = bf16[512,1024]{1,0:T(8,128)(2,1)} copy(bf16[512,1024]{1,0:T(8,128)(2,1)} %attention_block.1) | data formatting | bytes 2097152

commit v2 on v1

--- a/solution.py
+++ b/solution.py
@@ -152,11 +152,16 @@
         both("near", j, 0, 2, nxt)
         side("d1", j, 0, 1, c == 0)
 
-    def kv_mid(j):
-        both_recv("near", j, 2)
-        sm.go(f"fark{j}", slot(kd, j, 2), slot(kd, j, 4), nxt)
+    def kv_fwd(j):
         sm.remote(f"relay{j}", vrelay.at[j], vrelay.at[j], sib).wait_recv()
         sm.go(f"farv{j}", vrelay.at[j], slot(vd, j, 4), fwd)
+
+    def kv_mid(j):
+        sm.remote(f"neark{j}", slot(kd, j, 2), slot(kd, j, 2), sib).wait_recv()
+        sm.go(f"fark{j}", slot(kd, j, 2), slot(kd, j, 4), nxt)
+
+    def kv_side(j):
+        sm.remote(f"nearv{j}", slot(vd, j, 2), slot(vd, j, 2), sib).wait_recv()
         side("d1", j, 2, 1, c == 1)
         side("d2", j, 2, 3, c == 0)
 
@@ -231,131 +236,162 @@
         xcopy(2, h, xo, 0, 256, xp).wait_recv()
         xcopy(3, h, xo, 256, 256, xm).wait_recv()
 
-    wt = sm.remote("wt", w_ref, wbuf.at[c, y, z], swap)
-    wt_dst = sm.remote("wt", wbuf.at[c, y, z], wbuf.at[c, y, z], swap)
-    wl = pltpu.make_async_copy(w_ref, wbuf.at[c, y, z], loc_sem.at[12])
+    def half(ref, i):
+        return ref.at[pl.ds(512 * i, 512)]
+
+    def wt(i, src, dst):
+        return sm.remote(f"wt{i}", half(src, i), half(dst, i), swap)
+
+    def wl(i):
+        return pltpu.make_async_copy(half(w_ref, i), half(wbuf.at[c, y, z], i), loc_sem.at[12 + i])
 
     def w_swap():
         @pl.when(off)
         def _():
-            pltpu.make_async_remote_copy(
-                src_ref=w_ref, dst_ref=wbuf.at[c, mx, z], send_sem=send_sem.at[sm.index("wt")],
-                recv_sem=recv_sem.at[sm.index("wt")], device_id=swap, device_id_type=MESH).start()
+            for i in range(2):
+                wt(i, w_ref, wbuf.at[c, mx, z]).start()
 
         @pl.when(jnp.logical_not(off))
         def _():
-            wl.start()
-
-    def w_swapped():
+            for i in range(2):
+                wl(i).start()
+
+    def w_swapped(i):
         @pl.when(off)
         def _():
-            wt_dst.wait_recv()
+            wt(i, wbuf.at[c, y, z], wbuf.at[c, y, z]).wait_recv()
 
         @pl.when(jnp.logical_not(off))
         def _():
-            wl.wait()
+            wl(i).wait()
 
     def w_side(d1, d2):
         b = wblock(d1, d2)
         sm.go(f"ws{d1}{d2}", b, b, sib)
 
-    def w_send(d1, d2, second):
+    def w_send(d1, d2, second, halves=(0, 1)):
         b = wblock(d1, d2)
-        sm.go(f"w{second}+{d1}", b, b, along(not second, 1))
-        sm.go(f"w{second}-{d1}", b, b, along(not second, -1))
+        for i in halves:
+            for sign, k in (("+", i), ("-", 1 - i if len(halves) == 2 else i)):
+                sm.go(f"w{second}{sign}{d1}h{k}", half(b, k), half(b, k),
+                      along(not second, 1 if sign == "+" else -1))
+
+    def w_got(sign, d1, second, i, b):
+        sm.remote(f"w{second}{sign}{d1}h{i}", half(b, i), half(b, i), sib).wait_recv()
+
+    def w_pair(d1, second):
+        a, b = ((d1, -1), (d1, 1)) if second else ((-1, 0), (1, 0))
+        return a, b
 
     def w_relay(d1, second):
-        a, b = ((d1, -1), (d1, 1)) if second else ((-1, 0), (1, 0))
+        a, b = w_pair(d1, second)
         ra, rb = wblock(*a), wblock(*b)
-        sm.remote(f"w{second}+{d1}", ra, ra, sib).wait_recv()
-        h = ra.at[pl.ds(0, 512)]
-        sm.go(f"wr{second}+{d1}", h, h, along(not second, 1))
+        w_got("+", d1, second, 0, ra)
+        sm.go(f"wr{second}+{d1}", half(ra, 0), half(ra, 0), along(not second, 1))
+        w_got("-", d1, second, 1, rb)
+        sm.go(f"wr{second}-{d1}", half(rb, 1), half(rb, 1), along(not second, -1))
+
+    def w_rest(d1, second):
+        a, b = w_pair(d1, second)
+        w_got("+", d1, second, 1, wblock(*a))
         w_side(*a)
-        sm.remote(f"w{second}-{d1}", rb, rb, sib).wait_recv()
-        h = rb.at[pl.ds(512, 512)]
-        sm.go(f"wr{second}-{d1}", h, h, along(not second, -1))
+        w_got("-", d1, second, 0, wblock(*b))
         w_side(*b)
 
     def w_far(d1, second):
         o = (d1, 2) if second else (2, 0)
         b = wblock(*o)
-        sm.remote(f"wr{second}+{d1}", b.at[pl.ds(0, 512)], b.at[pl.ds(0, 512)], sib).wait_recv()
-        sm.remote(f"wr{second}-{d1}", b.at[pl.ds(512, 512)], b.at[pl.ds(512, 512)], sib).wait_recv()
+        sm.remote(f"wr{second}+{d1}", half(b, 0), half(b, 0), sib).wait_recv()
+        sm.remote(f"wr{second}-{d1}", half(b, 1), half(b, 1), sib).wait_recv()
         w_side(*o)
+
+    def project(block, js, init, last=False):
+        @pl.loop(0, 4)
+        def _(t):
+            cc, b = t // 2, (t % 2) * 2
+            hs = [j * 4 + g for j in js for g in range(4)]
+            a = jnp.concatenate([abuf[block, h] for h in hs], axis=1)
+            ks = pl.ds(js[0] * 512, 512 * len(js))
+            w = jnp.concatenate([wbuf[cc, block, b, ks, :], wbuf[cc, block, b + 1, ks, :]], axis=1)
+            o = jnp.dot(a, w, preferred_element_type=F32)
+            if not init:
+                o = o + oacc[t]
+            if last:
+                for i in range(2):
+                    cols = pl.ds(pl.multiple_of((2 * (b + i) + cc) * 128, 128), 128)
+                    out_ref[:, cols] = o[:, i * 128:(i + 1) * 128].astype(BF16)
+            else:
+                oacc[t] = o
 
     kv_near(0)
     w_swap()
     for d in lq:
         d.wait()
     sweep(0, 0)
+    kv_fwd(0)
     sweep(1, 0)
     kv_mid(0)
     kv_near(1)
-    w_swapped()
-    w_side(0, 0)
-    w_send(0, 0, 0)
-    w_send(0, 0, 1)
+    kv_side(0)
     both_recv("d1", 0, 1)
     sweep(0, 1)
+    kv_fwd(1)
+    w_swapped(0)
+    w_send(0, 0, 0, (0,))
     kv_last(0)
     both_recv("d2", 0, 3)
     sweep(0, 2, xsend)
+    w_swapped(1)
+    w_send(0, 0, 0, (1,))
+    w_side(0, 0)
     kv_mid(1)
+    kv_side(1)
+    w_send(0, 0, 1)
+    both_recv("d1", 1, 1)
+    sweep(1, 1)
     w_relay(0, 0)
+    w_rest(0, 0)
     w_send(-1, 0, 1)
     w_send(1, 0, 1)
-    both_recv("d1", 1, 1)
-    sweep(1, 1)
+    xrelay(0)
+    kv_last(1)
+    both_recv("d2", 1, 3)
+    sweep(1, 2, xsend)
     w_far(0, 0)
     w_send(2, 0, 1)
     w_relay(0, 1)
-    xrelay(0)
     xrelay(1)
-    kv_last(1)
-    both_recv("d2", 1, 3)
-    sweep(1, 2, xsend)
-
+    w_rest(0, 1)
     xrelay(2)
-    xrelay(3)
-    w_far(0, 1)
     w_relay(-1, 1)
     w_relay(1, 1)
+    xrelay(3)
+    w_rest(-1, 1)
+    w_rest(1, 1)
+    w_far(0, 1)
+    w_relay(2, 1)
     xrelay(4)
-    xrelay(5)
+    w_rest(2, 1)
     w_far(-1, 1)
     w_far(1, 1)
-    w_relay(2, 1)
+    xrelay(5)
+    w_far(2, 1)
+    for d1 in (0, -1, 1, 2):
+        for d2 in (0, -1, 1, 2):
+            sm.remote(f"ws{d1}{d2}", wbuf.at[1 - c, 0, 0], wbuf.at[1 - c, 0, 0], sib).wait_recv()
+    project(mx, (0, 1), True)
     xrelay(6)
+    project(xl, (0,), False)
+    project(xr, (0,), False)
     xrelay(7)
-    w_far(2, 1)
-    ws_dst = [(d1, d2) for d1 in (0, -1, 1, 2) for d2 in (0, -1, 1, 2)]
-    other = 1 - c
-    for d1, d2 in ws_dst:
-        sm.remote(f"ws{d1}{d2}", wbuf.at[other, 0, 0], wbuf.at[other, 0, 0], sib).wait_recv()
-
-    def project(block, j, init, last=False):
-        @pl.loop(0, 8)
-        def _(t):
-            cc, r = t // 4, pl.ds(pl.multiple_of((t % 4) * 128, 128), 128)
-            a = jnp.concatenate([abuf[block, j * 4 + g, r, :] for g in range(4)], axis=1)
-            w = jnp.concatenate([wbuf[cc, block, b, pl.ds(j * 512, 512), :] for b in range(4)], axis=1)
-            o = jnp.dot(a, w, preferred_element_type=F32)
-            if not init:
-                o = o + oacc[cc, r, :]
-            oacc[cc, r, :] = o
-
-    project(mx, 0, True)
-    project(mx, 1, False)
-    for j in range(2):
-        project(xl, j, False)
-        project(xr, j, False)
-    for h in range(8):
+    for h in range(4):
         xdone(h)
-    for j in range(2):
-        project(xo, j, False)
-    for cc in range(2):
-        for b in range(4):
-            out_ref[:, (2 * b + cc) * 128:(2 * b + cc + 1) * 128] = oacc[cc, :, b * 128:(b + 1) * 128].astype(BF16)
+    project(xo, (0,), False)
+    project(xl, (1,), False)
+    project(xr, (1,), False)
+    for h in range(4, 8):
+        xdone(h)
+    project(xo, (1,), False, True)
 
     for d in sm.pending:
         d.wait_send()
@@ -368,7 +404,8 @@
 
     @pl.when(off)
     def _():
-        wt.wait_send()
+        for i in range(2):
+            wt(i, w_ref, wbuf.at[c, mx, z]).wait_send()
     for h in range(8):
         xcopy(0, h, mx, 0, TOK, xp).wait_send()
         xcopy(1, h, mx, 0, TOK, xm).wait_send()
@@ -395,11 +432,11 @@
             pltpu.VMEM((4, 8, TOK, DH), BF16),
             pltpu.VMEM((8, TOK, DH), F32),
             pltpu.VMEM((8, TOK, 2 * DH), F32),
-            pltpu.VMEM((2, TOK, 512), F32),
+            pltpu.VMEM((4, TOK, 256), F32),
             pltpu.VMEM((8, DH), jnp.int32),
-            pltpu.SemaphoreType.DMA((13,)),
-            pltpu.SemaphoreType.DMA((64,)),
-            pltpu.SemaphoreType.DMA((64,)),
+            pltpu.SemaphoreType.DMA((14,)),
+            pltpu.SemaphoreType.DMA((96,)),
+            pltpu.SemaphoreType.DMA((96,)),
             pltpu.SemaphoreType.DMA((4, 8)),
             pltpu.SemaphoreType.DMA((4, 8)),
         ],

time: 88 us -> 76.6 us (0.87)
  Pallas kernels: 85.5 us -> 74.2 us
    pallas_call x1, Pallas kernels: 85.5 us -> 74.2 us  [body(): pl.pallas_call(kernel, out_shape=jax.ShapeDtypeStruct((TOK, 1024), BF16),...]
where the time goes in v2:
time: 76.6 us; the launch traced here: 76.4 us
  Pallas kernels  74.2 us (97%)
  local copies, waits for them, and re-layouts  2.26 us (3%)
    pallas_call x1, Pallas kernels, body(): pl.pallas_call(kernel, out_shape=jax.ShapeDtypeStruct((TOK, 1024), BF16),...  74.2 us
    unnamed x1, local copies, waits for them, and re-layouts  2.26 us

profile of v2, /device:TPU:1, one launch (start us, length us, event | category | flops | bytes accessed | tf_op | source)
XLA Modules:
  0.0 76.4 jit_solution(459096780898156101)
XLA Ops:
  0.0 74.2 %attention_block.1 = bf16[512,1024]{1,0:T(8,128)(2,1)} custom-call(bf16[512,1024]{1,0:T(8,128)(2,1)} %q_ref.1, bf16[512,256]{1,0:T(8,128)(2,1)} %k_ref.1, bf16[512,256]{1,0:T(8,128)(2,1)} %v_ref.1, bf16[1024,128]{1,0:T(8,128)(2,1)} %w_ref.1, s32[1,64]{1,0:T(1,128)} %bitcast.1), custom_call_target="tpu_custom_call" | custom-call | tf_op jit(solution)/shard_map/attention_block/pallas_call | solution.py:419
  74.2 2.3 %copy.7 = bf16[512,1024]{1,0:T(8,128)(2,1)} copy(bf16[512,1024]{1,0:T(8,128)(2,1)} %attention_block.1) | data formatting | bytes 2097152

commit v3 on v2

--- a/solution.py
+++ b/solution.py
@@ -30,14 +30,12 @@
             device_id=dev, device_id_type=MESH)
 
     def go(self, name, src, dst, dev):
-        d = self.remote(name, src, dst, dev)
-        d.start()
-        self.pending.append(d)
-        return d
+        self.remote(name, src, dst, dev).start()
+        self.pending.append((name, src.shape[0]))
 
 
 def kernel(q_ref, k_ref, v_ref, w_ref, len_ref, out_ref,
-           qd, qcode, kd, kcode, vd, vrelay, wbuf, abuf, mbuf, acc, oacc, lens,
+           qd, qcode, kd, kcode, vd, vrelay, wrelay, wbuf, abuf, mbuf, acc, oacc, lens,
            loc_sem, send_sem, recv_sem, xs_sem, xr_sem):
     mx = lax.axis_index("head")
     s = lax.axis_index("seq")
@@ -64,6 +62,9 @@
     bwd = dev(at(po // 4, (po + 3) % 4, c))
     swap = {"seq": at(mx, z, c), "head": y}
     off = mx != y
+    far, plus = (mx + 2) % 4 == y, mx == (y + 1) % 4
+    hop, unhop = {"seq": at((y + 3) % 4, z, c), "head": y}, {"seq": at((y + 1) % 4, z, c), "head": (mx + 2) % 4}
+    relays = plus
     f1, f2 = z + c * (y - z), y + c * (z - y)
 
     def along(first, step):
@@ -94,9 +95,17 @@
     for peer in (sib, nxt, prv, zp, zm, yp, ym, xp, xm, fwd, bwd):
         pl.semaphore_signal(barrier, inc=1, device_id=peer, device_id_type=MESH)
 
-    @pl.when(off)
+    @pl.when(off & jnp.logical_not(far))
     def _():
         pl.semaphore_signal(barrier, inc=1, device_id=swap, device_id_type=MESH)
+
+    @pl.when(far)
+    def _():
+        pl.semaphore_signal(barrier, inc=1, device_id=hop, device_id_type=MESH)
+
+    @pl.when(relays)
+    def _():
+        pl.semaphore_signal(barrier, inc=1, device_id=unhop, device_id_type=MESH)
 
     lens[...] = jnp.zeros_like(lens)
     lens[0:1, 0:64] = len_ref[...]
@@ -121,7 +130,7 @@
 
     for d in lk + lv:
         d.wait()
-    pl.semaphore_wait(barrier, 11 + off.astype(jnp.int32))
+    pl.semaphore_wait(barrier, 11 + off.astype(jnp.int32) + relays.astype(jnp.int32))
 
     def slot(buf, j, i):
         start_row = (4 - i) * TOK
@@ -200,7 +209,7 @@
             mbuf[h, rows, :] = new
             acc[h, rows, :] = o
 
-    def sweep(j, step, after=None):
+    def sweep(j, step, after=None, hooks=()):
         @pl.loop(0, 4)
         def _(g):
             h = j * 4 + g
@@ -213,6 +222,11 @@
                     tile(h, j, qc, 256 * qc, 1024 - 256 * qc, False, False, True)
             if after is not None:
                 after(h)
+            for when, steps in hooks:
+                @pl.when(g == when)
+                def _():
+                    for name, *args in steps:
+                        name(*args)
 
     def xcopy(kind, h, block, lo, n, to):
         ref = abuf.at[block, h, pl.ds(lo, n)]
@@ -236,8 +250,10 @@
         xcopy(2, h, xo, 0, 256, xp).wait_recv()
         xcopy(3, h, xo, 256, 256, xm).wait_recv()
 
+    parts = ((0, 512), (512, 512))
+
     def half(ref, i):
-        return ref.at[pl.ds(512 * i, 512)]
+        return ref.at[pl.ds(*parts[i])]
 
     def wt(i, src, dst):
         return sm.remote(f"wt{i}", half(src, i), half(dst, i), swap)
@@ -245,21 +261,44 @@
     def wl(i):
         return pltpu.make_async_copy(half(w_ref, i), half(wbuf.at[c, y, z], i), loc_sem.at[12 + i])
 
-    def w_swap():
-        @pl.when(off)
+
+    def w_hop(i, src):
+        return sm.remote(f"wh{i}", half(src, i), half(wrelay, i), hop)
+
+    def w_last(i, src):
+        return sm.remote(f"wz{i}", half(src, i), half(wbuf.at[c, (mx + 2) % 4, z], i), ym)
+
+    def w_swap(last):
+        @pl.when(plus if last else off & jnp.logical_not(plus | far))
         def _():
             for i in range(2):
                 wt(i, w_ref, wbuf.at[c, mx, z]).start()
 
-        @pl.when(jnp.logical_not(off))
-        def _():
-            for i in range(2):
-                wl(i).start()
+        if not last:
+            @pl.when(far)
+            def _():
+                for i in range(2):
+                    w_hop(i, w_ref).start()
+
+            @pl.when(jnp.logical_not(off))
+            def _():
+                for i in range(2):
+                    wl(i).start()
+
+    def w_passed(i):
+        @pl.when(relays)
+        def _():
+            w_hop(i, wrelay).wait_recv()
+            w_last(i, wrelay).start()
 
     def w_swapped(i):
-        @pl.when(off)
+        @pl.when(off & jnp.logical_not(far))
         def _():
             wt(i, wbuf.at[c, y, z], wbuf.at[c, y, z]).wait_recv()
+
+        @pl.when(far)
+        def _():
+            w_last(i, wrelay).wait_recv()
 
         @pl.when(jnp.logical_not(off))
         def _():
@@ -269,12 +308,24 @@
         b = wblock(d1, d2)
         sm.go(f"ws{d1}{d2}", b, b, sib)
 
-    def w_send(d1, d2, second, halves=(0, 1)):
+    def w_send(d1, d2, second, halves=(0, 1), core=None):
         b = wblock(d1, d2)
+        ds = []
         for i in halves:
             for sign, k in (("+", i), ("-", 1 - i if len(halves) == 2 else i)):
-                sm.go(f"w{second}{sign}{d1}h{k}", half(b, k), half(b, k),
-                      along(not second, 1 if sign == "+" else -1))
+                ds.append(sm.remote(f"w{second}{sign}{d1}h{k}", half(b, k), half(b, k),
+                                    along(not second, 1 if sign == "+" else -1)))
+                if core in (None, 0):
+                    sm.pending.append((f"w{second}{sign}{d1}h{k}", half(b, k).shape[0]))
+
+        def start():
+            for d in ds:
+                d.start()
+
+        if core is None:
+            start()
+        else:
+            pl.when(c == core)(start)
 
     def w_got(sign, d1, second, i, b):
         sm.remote(f"w{second}{sign}{d1}h{i}", half(b, i), half(b, i), sib).wait_recv()
@@ -305,96 +356,97 @@
         sm.remote(f"wr{second}-{d1}", half(b, 1), half(b, 1), sib).wait_recv()
         w_side(*o)
 
-    def project(block, js, init, last=False):
-        @pl.loop(0, 4)
-        def _(t):
-            cc, b = t // 2, (t % 2) * 2
-            hs = [j * 4 + g for j in js for g in range(4)]
-            a = jnp.concatenate([abuf[block, h] for h in hs], axis=1)
-            ks = pl.ds(js[0] * 512, 512 * len(js))
-            w = jnp.concatenate([wbuf[cc, block, b, ks, :], wbuf[cc, block, b + 1, ks, :]], axis=1)
-            o = jnp.dot(a, w, preferred_element_type=F32)
-            if not init:
-                o = o + oacc[t]
-            if last:
-                for i in range(2):
-                    cols = pl.ds(pl.multiple_of((2 * (b + i) + cc) * 128, 128), 128)
-                    out_ref[:, cols] = o[:, i * 128:(i + 1) * 128].astype(BF16)
-            else:
-                oacc[t] = o
+    def project(terms, init, last=False):
+        @pl.loop(0, 2)
+        def _(cc):
+            a = jnp.concatenate([abuf[x, j * 4 + g] for x, j in terms for g in range(4)], axis=1)
+            for b in (0, 2):
+                w = jnp.concatenate(
+                    [jnp.concatenate([wbuf[cc, x, b, pl.ds(j * 512, 512), :],
+                                      wbuf[cc, x, b + 1, pl.ds(j * 512, 512), :]], axis=1)
+                     for x, j in terms], axis=0)
+                o = jnp.dot(a, w, preferred_element_type=F32)
+                if not init:
+                    o = o + oacc[cc, b // 2]
+                if last:
+                    for i in range(2):
+                        cols = pl.ds(pl.multiple_of((2 * (b + i) + cc) * 128, 128), 128)
+                        out_ref[:, cols] = o[:, i * 128:(i + 1) * 128].astype(BF16)
+                else:
+                    oacc[cc, b // 2] = o
 
     kv_near(0)
-    w_swap()
+    w_swap(False)
     for d in lq:
         d.wait()
     sweep(0, 0)
-    kv_fwd(0)
     sweep(1, 0)
     kv_mid(0)
-    kv_near(1)
+    kv_fwd(0)
+    w_swap(True)
     kv_side(0)
     both_recv("d1", 0, 1)
     sweep(0, 1)
-    kv_fwd(1)
-    w_swapped(0)
-    w_send(0, 0, 0, (0,))
+    w_passed(0)
+    w_passed(1)
+    kv_near(1)
     kv_last(0)
     both_recv("d2", 0, 3)
     sweep(0, 2, xsend)
+    w_swapped(0)
     w_swapped(1)
-    w_send(0, 0, 0, (1,))
+    w_send(0, 0, 0)
+    w_send(0, 0, 1, (0, 1), 0)
     w_side(0, 0)
+    kv_fwd(1)
     kv_mid(1)
     kv_side(1)
-    w_send(0, 0, 1)
     both_recv("d1", 1, 1)
-    sweep(1, 1)
-    w_relay(0, 0)
-    w_rest(0, 0)
-    w_send(-1, 0, 1)
-    w_send(1, 0, 1)
-    xrelay(0)
+    sweep(1, 1, None, (
+        (2, ((w_relay, 0, 0), (w_rest, 0, 0),
+             (w_send, 1, 0, 1, (0, 1), 0), (w_send, -1, 0, 1, (0, 1), 0),
+             (w_send, 0, 0, 1, (0, 1), 1), (w_send, 1, 0, 1, (0, 1), 1), (w_send, -1, 0, 1, (0, 1), 1))),
+        (3, ((xrelay, 0),)),
+    ))
     kv_last(1)
     both_recv("d2", 1, 3)
-    sweep(1, 2, xsend)
-    w_far(0, 0)
-    w_send(2, 0, 1)
+    sweep(1, 2, xsend, (
+        (0, ((w_far, 0, 0), (w_send, 2, 0, 1))),
+        (1, ((xrelay, 1),)),
+        (3, ((xrelay, 2),)),
+    ))
     w_relay(0, 1)
-    xrelay(1)
-    w_rest(0, 1)
-    xrelay(2)
-    w_relay(-1, 1)
     w_relay(1, 1)
     xrelay(3)
+    w_relay(-1, 1)
+    xrelay(4)
+    w_rest(0, 1)
+    w_rest(1, 1)
     w_rest(-1, 1)
-    w_rest(1, 1)
+    xrelay(5)
+    w_relay(2, 1)
+    xrelay(6)
     w_far(0, 1)
-    w_relay(2, 1)
-    xrelay(4)
     w_rest(2, 1)
+    xrelay(7)
+    w_far(1, 1)
     w_far(-1, 1)
-    w_far(1, 1)
-    xrelay(5)
     w_far(2, 1)
     for d1 in (0, -1, 1, 2):
         for d2 in (0, -1, 1, 2):
             sm.remote(f"ws{d1}{d2}", wbuf.at[1 - c, 0, 0], wbuf.at[1 - c, 0, 0], sib).wait_recv()
-    project(mx, (0, 1), True)
-    xrelay(6)
-    project(xl, (0,), False)
-    project(xr, (0,), False)
-    xrelay(7)
+    project([(mx, 0), (mx, 1)], True)
+    project([(xl, 0), (xr, 0)], False)
     for h in range(4):
         xdone(h)
-    project(xo, (0,), False)
-    project(xl, (1,), False)
-    project(xr, (1,), False)
+    project([(xo, 0), (xl, 1), (xr, 1)], False)
     for h in range(4, 8):
         xdone(h)
-    project(xo, (1,), False, True)
-
-    for d in sm.pending:
-        d.wait_send()
+    project([(xo, 1)], False, True)
+
+    for name, n in sm.pending:
+        ref = wrelay.at[pl.ds(0, n)]
+        sm.remote(name, ref, ref, sib).wait_send()
     for j in range(2):
         for kv in "kv":
             buf = kd if kv == "k" else vd
@@ -404,8 +456,20 @@
 
     @pl.when(off)
     def _():
+        @pl.when(jnp.logical_not(far))
+        def _():
+            for i in range(2):
+                wt(i, w_ref, wbuf.at[c, mx, z]).wait_send()
+
+    @pl.when(far)
+    def _():
         for i in range(2):
-            wt(i, w_ref, wbuf.at[c, mx, z]).wait_send()
+            w_hop(i, w_ref).wait_send()
+
+    @pl.when(relays)
+    def _():
+        for i in range(2):
+            w_last(i, wrelay).wait_send()
     for h in range(8):
         xcopy(0, h, mx, 0, TOK, xp).wait_send()
         xcopy(1, h, mx, 0, TOK, xm).wait_send()
@@ -428,11 +492,12 @@
             pltpu.VMEM((ROWS, DH), BF16),
             pltpu.VMEM((2, ROWS, DH), BF16),
             pltpu.VMEM((2, TOK, DH), BF16),
+            pltpu.VMEM((1024, DH), BF16),
             pltpu.VMEM((2, 4, 4, 1024, DH), BF16),
             pltpu.VMEM((4, 8, TOK, DH), BF16),
             pltpu.VMEM((8, TOK, DH), F32),
             pltpu.VMEM((8, TOK, 2 * DH), F32),
-            pltpu.VMEM((4, TOK, 256), F32),
+            pltpu.VMEM((2, 2, TOK, 256), F32),
             pltpu.VMEM((8, DH), jnp.int32),
             pltpu.SemaphoreType.DMA((14,)),
             pltpu.SemaphoreType.DMA((96,)),

time: 76.6 us -> 71.9 us (0.939)
  Pallas kernels: 74.2 us -> 69.5 us
    pallas_call x1, Pallas kernels: 74.2 us -> 69.5 us  [body(): pl.pallas_call(kernel, out_shape=jax.ShapeDtypeStruct((TOK, 1024), BF16),...]
where the time goes in v3:
time: 71.9 us; the launch traced here: 71.8 us
  Pallas kernels  69.5 us (97%)
  local copies, waits for them, and re-layouts  2.26 us (3%)
    pallas_call x1, Pallas kernels, body(): pl.pallas_call(kernel, out_shape=jax.ShapeDtypeStruct((TOK, 1024), BF16),...  69.5 us
    unnamed x1, local copies, waits for them, and re-layouts  2.26 us

profile of v3, /device:TPU:1, one launch (start us, length us, event | category | flops | bytes accessed | tf_op | source)
XLA Modules:
  0.0 71.8 jit_solution(320419796523987796)
XLA Ops:
  0.0 69.5 %attention_block.1 = bf16[512,1024]{1,0:T(8,128)(2,1)} custom-call(bf16[512,1024]{1,0:T(8,128)(2,1)} %q_ref.1, bf16[512,256]{1,0:T(8,128)(2,1)} %k_ref.1, bf16[512,256]{1,0:T(8,128)(2,1)} %v_ref.1, bf16[1024,128]{1,0:T(8,128)(2,1)} %w_ref.1, s32[1,64]{1,0:T(1,128)} %bitcast.1), custom_call_target="tpu_custom_call" | custom-call | tf_op jit(solution)/shard_map/attention_block/pallas_call | solution.py:483
  69.5 2.3 %copy.7 = bf16[512,1024]{1,0:T(8,128)(2,1)} copy(bf16[512,1024]{1,0:T(8,128)(2,1)} %attention_block.1) | data formatting | bytes 2097152

commit v4 on v3

--- a/solution.py
+++ b/solution.py
@@ -31,11 +31,11 @@
 
     def go(self, name, src, dst, dev):
         self.remote(name, src, dst, dev).start()
-        self.pending.append((name, src.shape[0]))
+        self.pending.append((name, src.shape[0] * src.shape[1] // DH))
 
 
 def kernel(q_ref, k_ref, v_ref, w_ref, len_ref, out_ref,
-           qd, qcode, kd, kcode, vd, vrelay, wrelay, wbuf, abuf, mbuf, acc, oacc, lens,
+           qd, qcode, kd, kcode, vown, vd, vrelay, wrelay, wbuf, abuf, mbuf, acc, s0, s1, s2, s3, t0, t1, t2, t3, oacc, lens,
            loc_sem, send_sem, recv_sem, xs_sem, xr_sem):
     mx = lax.axis_index("head")
     s = lax.axis_index("seq")
@@ -88,7 +88,7 @@
 
     own = pl.ds(2048, TOK)
     lk = [local(k_ref.at[:, pl.ds(j * DH, DH)], kd.at[j, own]) for j in range(2)]
-    lv = [local(v_ref.at[:, pl.ds(j * DH, DH)], vd.at[j, own]) for j in range(2)]
+    lv = [local(v_ref.at[:, pl.ds(j * DH, DH)], vown.at[j]) for j in range(2)]
     lq = [local(q_ref.at[:, pl.ds(h * DH, DH)], qd.at[h]) for h in range(8)]
 
     barrier = pltpu.get_barrier_semaphore()
@@ -130,9 +130,13 @@
 
     for d in lk + lv:
         d.wait()
+    for j in range(2):
+        vd[j, 4] = vown[j].T
     pl.semaphore_wait(barrier, 11 + off.astype(jnp.int32) + relays.astype(jnp.int32))
 
     def slot(buf, j, i):
+        if buf is vd:
+            return vd.at[j, 4 - i]
         start_row = (4 - i) * TOK
         if not isinstance(i, int):
             start_row = pl.multiple_of(start_row, TOK)
@@ -179,52 +183,75 @@
         sm.remote(f"farv{j}", slot(vd, j, 4), slot(vd, j, 4), sib).wait_recv()
         side("d2", j, 4, 3, c == 1)
 
-    ones = jnp.ones((256, DH), BF16)
-
-    def tile(h, j, qc, lo, n, init, diag, last):
+    CK, WK = 1024, 256
+
+    def scores(h, j, qc, lo, n, diag, sref, tref):
         rows = pl.ds(qc * 256, 256)
         qa = jnp.concatenate([qd[h, rows, :], qcode[rows, :]], axis=1)
-        ka = jnp.concatenate([kd[j, pl.ds(lo, n), :], kcode[pl.ds(lo, n), :]], axis=1)
-        sc = lax.dot_general(qa, ka, (((1,), (1,)), ((), ())), preferred_element_type=F32)
-        if diag:
-            r = lax.broadcasted_iota(jnp.int32, (256, n), 0)
-            u = lax.broadcasted_iota(jnp.int32, (256, n), 1)
-            sc = jnp.where(u <= r + qc * 256, sc, -FAR)
-        top = jnp.max(sc, axis=1, keepdims=True)
-        if init:
-            new = jnp.broadcast_to(top, (256, DH))
+        top = None
+        for at_key in range(0, n, CK):
+            m = min(CK, n - at_key)
+            keys = pl.ds(lo + at_key, m)
+            ka = jnp.concatenate([kd[j, keys, :], kcode[keys, :]], axis=1)
+            sc = lax.dot_general(ka, qa, (((1,), (1,)), ((), ())), preferred_element_type=F32)
+            if diag:
+                u = at_key + lax.broadcasted_iota(jnp.int32, (m, 256), 0)
+                r = lax.broadcasted_iota(jnp.int32, (m, 256), 1)
+                sc = jnp.where(u <= r + qc * 256, sc, -FAR)
+            sref[at_key:at_key + m, :] = sc
+            best = jnp.max(sc.reshape(m // 8, 8, 256), axis=0)
+            top = best if top is None else jnp.maximum(top, best)
+            yield
+        tref[...] = jnp.broadcast_to(jnp.max(top, axis=0, keepdims=True), (8, 256))
+
+    def weigh(h, j, qc, lo, n, init, last, sref, tref):
+        rows = pl.ds(qc * 256, 256)
+        new = tref[0:1, :]
+        if not init:
+            old = mbuf[h, qc, 0:1, :]
+            new = jnp.maximum(old, new)
+            o = acc[h, qc] * jnp.exp2((old - new) * C2)
+        at_key = lo
+        while at_key < lo + n:
+            m = min(WK, lo + n - at_key, TOK - at_key % TOK)
+            pr = jnp.exp2((sref[pl.ds(at_key - lo, m), :] - new) * C2).astype(BF16)
+            va = jnp.concatenate(
+                [vd[j, at_key // TOK, :, pl.ds(at_key % TOK, m)], jnp.ones((16, m), BF16)], axis=0)
+            part = jnp.dot(va, pr, preferred_element_type=F32)
+            o = part if init and at_key == lo else o + part
+            at_key += m
+            yield
+        if last:
+            abuf[mx, h, rows, :] = (o[:DH] / o[DH:DH + 1]).T.astype(BF16)
         else:
-            old = mbuf[h, rows, :]
-            new = jnp.maximum(old, top)
-        pr = jnp.exp2((sc - jnp.concatenate([new] * (n // DH), axis=1)) * C2).astype(BF16)
-        va = jnp.concatenate(
-            [vd[j, pl.ds(lo, n), :], jnp.concatenate([ones] * (n // 256), axis=0)], axis=1)
-        o = jnp.dot(pr, va, preferred_element_type=F32)
-        if not init:
-            fade = jnp.exp2((old - new) * C2)
-            o = o + acc[h, rows, :] * jnp.concatenate([fade, fade], axis=1)
-        if last:
-            abuf[mx, h, rows, :] = (o[:, :DH] / o[:, DH:]).astype(BF16)
-        else:
-            mbuf[h, rows, :] = new
-            acc[h, rows, :] = o
+            mbuf[h, qc] = jnp.broadcast_to(new, (8, 256))
+            acc[h, qc] = o
+
+    def interleave(*streams):
+        live = list(streams)
+        while live:
+            live = [s for s in live if next(s, live) is not live]
 
     def sweep(j, step, after=None, hooks=()):
-        @pl.loop(0, 4)
-        def _(g):
-            h = j * 4 + g
-            for qc in range(2):
-                if step == 0:
-                    tile(h, j, qc, 2048, 256 + 256 * qc, True, True, False)
-                elif step == 1:
-                    tile(h, j, qc, 1024, 1024, False, False, False)
-                else:
-                    tile(h, j, qc, 256 * qc, 1024 - 256 * qc, False, False, True)
+        init, last = step == 0, step == 2
+        spans = {0: ((2048, 256), (2048, 512)), 1: ((1024, 1024), (1024, 1024)), 2: ((0, 1024), (256, 768))}[step]
+        bufs = ((s0, s1), (s2, s3)), ((t0, t1), (t2, t3))
+
+        def make(g):
+            return [scores(j * 4 + g, j, qc, *spans[qc], init, bufs[0][g % 2][qc], bufs[1][g % 2][qc])
+                    for qc in range(2)]
+
+        def use(g):
+            return [weigh(j * 4 + g, j, qc, *spans[qc], init, last, bufs[0][g % 2][qc], bufs[1][g % 2][qc])
+                    for qc in range(2)]
+
+        interleave(*make(0))
+        for g in range(4):
+            interleave(*(make(g + 1) if g < 3 else []), *use(g))
             if after is not None:
-                after(h)
+                after(j * 4 + g)
             for when, steps in hooks:
-                @pl.when(g == when)
-                def _():
+                if when == g:
                     for name, *args in steps:
                         name(*args)
 
@@ -383,8 +410,8 @@
     sweep(1, 0)
     kv_mid(0)
     kv_fwd(0)
+    kv_side(0)
     w_swap(True)
-    kv_side(0)
     both_recv("d1", 0, 1)
     sweep(0, 1)
     w_passed(0)
@@ -482,7 +509,7 @@
     vmem = pl.BlockSpec(memory_space=pltpu.VMEM)
     return pl.pallas_call(
         kernel,
-        out_shape=jax.ShapeDtypeStruct((TOK, 1024), BF16),
+        out_shape=pltpu.VMEM((TOK, 1024), BF16),
         in_specs=[hbm, hbm, hbm, hbm, vmem],
         out_specs=vmem,
         scratch_shapes=[
@@ -490,13 +517,16 @@
             pltpu.VMEM((TOK, DH), BF16),
             pltpu.VMEM((2, ROWS, DH), BF16),
             pltpu.VMEM((ROWS, DH), BF16),
-            pltpu.VMEM((2, ROWS, DH), BF16),
             pltpu.VMEM((2, TOK, DH), BF16),
+            pltpu.VMEM((2, 5, DH, TOK), BF16),
+            pltpu.VMEM((2, DH, TOK), BF16),
             pltpu.VMEM((1024, DH), BF16),
             pltpu.VMEM((2, 4, 4, 1024, DH), BF16),
             pltpu.VMEM((4, 8, TOK, DH), BF16),
-            pltpu.VMEM((8, TOK, DH), F32),
-            pltpu.VMEM((8, TOK, 2 * DH), F32),
+            pltpu.VMEM((8, 2, 8, 256), F32),
+            pltpu.VMEM((8, 2, DH + 16, 256), F32),
+            *[pltpu.VMEM((1024, 256), F32)] * 4,
+            *[pltpu.VMEM((8, 256), F32)] * 4,
             pltpu.VMEM((2, 2, TOK, 256), F32),
             pltpu.VMEM((8, DH), jnp.int32),
             pltpu.SemaphoreType.DMA((14,)),

time: 71.9 us -> 68.5 us (0.953)
  Pallas kernels: 69.5 us -> 67.4 us
  local copies, waits for them, and re-layouts: 2.26 us -> 0.97 us
    pallas_call x1, Pallas kernels: 69.5 us -> 67.4 us  [body(): pl.pallas_call(kernel, out_shape=pltpu.VMEM((TOK, 1024), BF16), in_specs=...]
    unnamed x1, local copies, waits for them, and re-layouts: 2.26 us -> 0.97 us
where the time goes in v4:
time: 68.5 us; the launch traced here: 68.4 us
  Pallas kernels  67.4 us (98%)
  local copies, waits for them, and re-layouts  0.97 us (1%)
    pallas_call x1, Pallas kernels, body(): pl.pallas_call(kernel, out_shape=pltpu.VMEM((TOK, 1024), BF16), in_specs=...  67.4 us

profile of v4, /device:TPU:1, one launch (start us, length us, event | category | flops | bytes accessed | tf_op | source)
XLA Modules:
  0.0 68.4 jit_solution(17914802307264812270)
XLA Ops:
  0.0 67.4 %attention_block.1 = bf16[512,1024]{1,0:T(8,128)(2,1)S(1)} custom-call(bf16[512,1024]{1,0:T(8,128)(2,1)} %q_ref.1, bf16[512,256]{1,0:T(8,128)(2,1)} %k_ref.1, bf16[512,256]{1,0:T(8,128)(2,1)} %v_ref.1, bf16[1024,128]{1,0:T(8,128)(2,1)} %w_ref.1, s32[1,64]{1,0:T(1,128)} %bitcast.1), custom_call_target="tpu_custom_call" | custom-call | tf_op jit(solution)/shard_map/attention_block/pallas_call | solution.py:510
  67.4 1.0 %copy.7 = bf16[512,1024]{1,0:T(8,128)(2,1)} copy(bf16[512,1024]{1,0:T(8,128)(2,1)S(1)} %attention_block.1) | data formatting | bytes 2097152

commit v5 on v4

--- a/solution.py
+++ b/solution.py
@@ -383,24 +383,27 @@
         sm.remote(f"wr{second}-{d1}", half(b, 1), half(b, 1), sib).wait_recv()
         w_side(*o)
 
+    def project_one(cc, terms, init, last=False):
+        a = jnp.concatenate([abuf[x, j * 4 + g] for x, j in terms for g in range(4)], axis=1)
+        for b in (0, 2):
+            w = jnp.concatenate(
+                [jnp.concatenate([wbuf[cc, x, b, pl.ds(j * 512, 512), :],
+                                  wbuf[cc, x, b + 1, pl.ds(j * 512, 512), :]], axis=1)
+                 for x, j in terms], axis=0)
+            o = jnp.dot(a, w, preferred_element_type=F32)
+            if not init:
+                o = o + oacc[cc, b // 2]
+            if last:
+                for i in range(2):
+                    cols = pl.ds(pl.multiple_of((2 * (b + i) + cc) * 128, 128), 128)
+                    out_ref[:, cols] = o[:, i * 128:(i + 1) * 128].astype(BF16)
+            else:
+                oacc[cc, b // 2] = o
+
     def project(terms, init, last=False):
         @pl.loop(0, 2)
         def _(cc):
-            a = jnp.concatenate([abuf[x, j * 4 + g] for x, j in terms for g in range(4)], axis=1)
-            for b in (0, 2):
-                w = jnp.concatenate(
-                    [jnp.concatenate([wbuf[cc, x, b, pl.ds(j * 512, 512), :],
-                                      wbuf[cc, x, b + 1, pl.ds(j * 512, 512), :]], axis=1)
-                     for x, j in terms], axis=0)
-                o = jnp.dot(a, w, preferred_element_type=F32)
-                if not init:
-                    o = o + oacc[cc, b // 2]
-                if last:
-                    for i in range(2):
-                        cols = pl.ds(pl.multiple_of((2 * (b + i) + cc) * 128, 128), 128)
-                        out_ref[:, cols] = o[:, i * 128:(i + 1) * 128].astype(BF16)
-                else:
-                    oacc[cc, b // 2] = o
+            project_one(cc, terms, init, last)
 
     kv_near(0)
     w_swap(False)
@@ -411,23 +414,23 @@
     kv_mid(0)
     kv_fwd(0)
     kv_side(0)
+    kv_near(1)
     w_swap(True)
     both_recv("d1", 0, 1)
     sweep(0, 1)
     w_passed(0)
     w_passed(1)
-    kv_near(1)
     kv_last(0)
     both_recv("d2", 0, 3)
     sweep(0, 2, xsend)
+    kv_fwd(1)
+    kv_mid(1)
     w_swapped(0)
     w_swapped(1)
     w_send(0, 0, 0)
     w_send(0, 0, 1, (0, 1), 0)
+    kv_side(1)
     w_side(0, 0)
-    kv_fwd(1)
-    kv_mid(1)
-    kv_side(1)
     both_recv("d1", 1, 1)
     sweep(1, 1, None, (
         (2, ((w_relay, 0, 0), (w_rest, 0, 0),
@@ -450,23 +453,25 @@
     w_rest(0, 1)
     w_rest(1, 1)
     w_rest(-1, 1)
+    w_far(0, 1)
     xrelay(5)
     w_relay(2, 1)
+    w_far(1, 1)
+    w_rest(2, 1)
+    w_far(-1, 1)
     xrelay(6)
-    w_far(0, 1)
-    w_rest(2, 1)
+    w_far(2, 1)
     xrelay(7)
-    w_far(1, 1)
-    w_far(-1, 1)
-    w_far(2, 1)
+    for h in range(4):
+        xdone(h)
+    project_one(c, [(mx, 0), (mx, 1)], True)
+    project_one(c, [(xl, 0), (xr, 0), (xo, 0)], False)
     for d1 in (0, -1, 1, 2):
         for d2 in (0, -1, 1, 2):
             sm.remote(f"ws{d1}{d2}", wbuf.at[1 - c, 0, 0], wbuf.at[1 - c, 0, 0], sib).wait_recv()
-    project([(mx, 0), (mx, 1)], True)
-    project([(xl, 0), (xr, 0)], False)
-    for h in range(4):
-        xdone(h)
-    project([(xo, 0), (xl, 1), (xr, 1)], False)
+    project_one(1 - c, [(mx, 0), (mx, 1)], True)
+    project_one(1 - c, [(xl, 0), (xr, 0), (xo, 0)], False)
+    project([(xl, 1), (xr, 1)], False)
     for h in range(4, 8):
         xdone(h)
     project([(xo, 1)], False, True)

time: 68.5 us -> 64.7 us (0.945)
  Pallas kernels: 67.4 us -> 63.6 us
    pallas_call x1, Pallas kernels: 67.4 us -> 63.6 us  [body(): pl.pallas_call(kernel, out_shape=pltpu.VMEM((TOK, 1024), BF16), in_specs=...]
where the time goes in v5:
time: 64.7 us; the launch traced here: 64.5 us
  Pallas kernels  63.6 us (98%)
  local copies, waits for them, and re-layouts  0.97 us (1%)
    pallas_call x1, Pallas kernels, body(): pl.pallas_call(kernel, out_shape=pltpu.VMEM((TOK, 1024), BF16), in_specs=...  63.6 us

profile of v5, /device:TPU:1, one launch (start us, length us, event | category | flops | bytes accessed | tf_op | source)
XLA Modules:
  0.0 64.5 jit_solution(2183329888427304168)
XLA Ops:
  0.0 63.6 %attention_block.1 = bf16[512,1024]{1,0:T(8,128)(2,1)S(1)} custom-call(bf16[512,1024]{1,0:T(8,128)(2,1)} %q_ref.1, bf16[512,256]{1,0:T(8,128)(2,1)} %k_ref.1, bf16[512,256]{1,0:T(8,128)(2,1)} %v_ref.1, bf16[1024,128]{1,0:T(8,128)(2,1)} %w_ref.1, s32[1,64]{1,0:T(1,128)} %bitcast.1), custom_call_target="tpu_custom_call" | custom-call | tf_op jit(solution)/shard_map/attention_block/pallas_call | solution.py:515
  63.6 1.0 %copy.7 = bf16[512,1024]{1,0:T(8,128)(2,1)} copy(bf16[512,1024]{1,0:T(8,128)(2,1)S(1)} %attention_block.1) | data formatting | bytes 2097152

commit v6 on v5

--- a/solution.py
+++ b/solution.py
@@ -438,30 +438,30 @@
              (w_send, 0, 0, 1, (0, 1), 1), (w_send, 1, 0, 1, (0, 1), 1), (w_send, -1, 0, 1, (0, 1), 1))),
         (3, ((xrelay, 0),)),
     ))
+    xrelay(1)
     kv_last(1)
     both_recv("d2", 1, 3)
     sweep(1, 2, xsend, (
         (0, ((w_far, 0, 0), (w_send, 2, 0, 1))),
-        (1, ((xrelay, 1),)),
-        (3, ((xrelay, 2),)),
+        (1, ((xrelay, 2),)),
     ))
     w_relay(0, 1)
     w_relay(1, 1)
     xrelay(3)
     w_relay(-1, 1)
     xrelay(4)
+    w_relay(2, 1)
     w_rest(0, 1)
     w_rest(1, 1)
     w_rest(-1, 1)
+    xrelay(5)
     w_far(0, 1)
-    xrelay(5)
-    w_relay(2, 1)
     w_far(1, 1)
     w_rest(2, 1)
+    xrelay(6)
     w_far(-1, 1)
-    xrelay(6)
+    xrelay(7)
     w_far(2, 1)
-    xrelay(7)
     for h in range(4):
         xdone(h)
     project_one(c, [(mx, 0), (mx, 1)], True)

time: 64.7 us -> 64.3 us (level); the launches traced: 64.5 us -> 63.2 us
  Pallas kernels: 63.6 us -> 62.2 us
    pallas_call x1, Pallas kernels: 63.6 us -> 62.2 us  [body(): pl.pallas_call(kernel, out_shape=pltpu.VMEM((TOK, 1024), BF16), in_specs=...]
where the time goes in v6:
time: 64.3 us; the launch traced here: 63.2 us
  Pallas kernels  62.2 us (97%)
  local copies, waits for them, and re-layouts  0.97 us (2%)
    pallas_call x1, Pallas kernels, body(): pl.pallas_call(kernel, out_shape=pltpu.VMEM((TOK, 1024), BF16), in_specs=...  62.2 us

profile of v6, /device:TPU:1, one launch (start us, length us, event | category | flops | bytes accessed | tf_op | source)
XLA Modules:
  0.0 63.2 jit_solution(2174574649571377538)
XLA Ops:
  0.0 62.2 %attention_block.1 = bf16[512,1024]{1,0:T(8,128)(2,1)S(1)} custom-call(bf16[512,1024]{1,0:T(8,128)(2,1)} %q_ref.1, bf16[512,256]{1,0:T(8,128)(2,1)} %k_ref.1, bf16[512,256]{1,0:T(8,128)(2,1)} %v_ref.1, bf16[1024,128]{1,0:T(8,128)(2,1)} %w_ref.1, s32[1,64]{1,0:T(1,128)} %bitcast.1), custom_call_target="tpu_custom_call" | custom-call | tf_op jit(solution)/shard_map/attention_block/pallas_call | solution.py:515
  62.2 1.0 %copy.7 = bf16[512,1024]{1,0:T(8,128)(2,1)} copy(bf16[512,1024]{1,0:T(8,128)(2,1)S(1)} %attention_block.1) | data formatting | bytes 2097152
